TPU v7x, 32 devices: a whole 2x2x4 slice. The times are simulated.
32 devices in a mesh: row: 8 (over z, y), col: 4 (over x, core).
Axes of the slice: x: 2, y: 2, z: 4, core: 2. Of those that a mesh axis runs over, the one named last changes fastest.
Arguments:
- lower_panel: float32 [1, 4, 512, 4096], P(None, None, 'col', 'row'), may hold values from -4 to 4, as said below
- right_side: float32 [1, 4096, 4096], P(None, 'row', 'col'), may hold values from -6 to 6
Outputs:
- solution: float32 [4, 512, 4096], P(None, None, 'col')
- updated_rhs: float32 [1, 4096, 4096], P(None, 'row', 'col')
Inputs may be any that keep to these rules, and one draw needn't show every extreme that they name: `lower_panel`: L is lower triangular: entries of tiles L[g, s] with g < s and above the diagonal of L[s, s] are zero; the diagonal entries of L lie between 2 and 4.
All inputs are finite; a program needn't handle non-finite values.
Results may differ from a plain program's by a relative error of at most 0.00017.
Values sent between devices are 32-bit elements; how exact they have to be, the bound alone decides.
A program may use at most 128 MiB of HBM per device.

v0:
```python
import jax
import jax.numpy as jnp
from jax import lax
from jax.sharding import PartitionSpec as P


def from_root(x, axis, root):
    mine = lax.axis_index(axis) == root
    return lax.psum(jnp.where(mine, x, jnp.zeros_like(x)), axis)


def per_device(lower_panel, right_side):
    rounds = lower_panel.shape[0]
    sections = lower_panel.shape[1]
    block = lower_panel.shape[3]
    my_row = lax.axis_index("row")
    row_count = lax.axis_size("row")
    tile_number = jnp.arange(rounds, dtype=jnp.int32) * row_count + my_row
    current = right_side
    collected = []
    for section in range(sections):
        is_owner = my_row == section
        column = lax.dynamic_index_in_dim(lower_panel, section, 1, keepdims=False)
        diag_tile = lax.all_gather(column[0], "col", axis=0, tiled=True).T
        safe_tile = jnp.where(is_owner, diag_tile, jnp.eye(block, dtype=jnp.float32))
        local_solve = lax.linalg.triangular_solve(safe_tile, current[0], left_side=True, lower=True)
        solved = from_root(local_solve, "row", section)
        rows_here = solved
        update = jnp.einsum(
            "rcq,cx->rqx",
            lax.all_gather(column, "col", axis=1, tiled=True),
            rows_here,
            precision=lax.Precision.HIGHEST,
        )
        keep_rows = (tile_number > section)[:, None, None]
        current, solved = (current - jnp.where(keep_rows, update, jnp.float32(0.0)), solved)
        collected.append(solved)
    solutions = jnp.stack(collected)
    return (solutions, current)


def solution(mesh):
    placed = (P(None, None, "col", "row"), P(None, "row", "col"))
    return jax.shard_map(
        per_device,
        mesh=mesh,
        in_specs=placed,
        out_specs=(P(None, None, "col"), P(None, "row", "col")),
        check_vma=False,
    )
```

profile of v0, /device:TPU:0, one launch (start us, length us, event | category | flops | bytes accessed | tf_op | source)
XLA Modules:
  0.0 589.0 jit_solution(5360135936811088487)
XLA Ops:
  7.2 2.0 fusion.100
  9.2 0.8 copy.10
  10.1 0.8 copy.11
  11.1 18.7 %all-gather.13.cloned.1.call-done = f32[1,1,512,512]{2,3,1,0:T(8,128)} async-done(((f32[1,1,128,512]{2,3,1,0:T(8,128)}), f32[1,1,512,512]{2,3,1,0:T(8,128)}) %all-gather.13.cloned.1.call-update) | async-done | bytes 1048592 | tf_op jit(solution)/shard_map/all_gather | solution.py:24
  29.8 1.4 fusion.36
  31.1 0.7 broadcast.74.clone
  31.9 10.0 %while.8 = (s32[]{:T(128)}, f32[512,512]{1,0:T(8,128)S(1)}, s32[4,2]{0,1:T(2,128)S(1)}, f32[4,128,128]{2,1,0:T(8,128)}, s32[]{:T(128)}) while((s32[]{:T(128)}, f32[512,512]{1,0:T(8,128)S(1)}, s32[4,2]{0,1:T(2,128)S(1)}, f32[4,128,128]{2,1,0:T(8,128)}, s32[]{:T(128)}) %tuple.71), condition=%wide.while_cond, body=%wide.while_body.sunk | while | flops 2 | bytes 132205 | solution.py:26
  32.5 1.9 bitcast_dynamic-update-slice_fusion.8
  34.9 1.9 bitcast_dynamic-update-slice_fusion.8
  37.4 1.9 bitcast_dynamic-update-slice_fusion.8
  39.9 1.9 bitcast_dynamic-update-slice_fusion.8
  41.8 40.7 %custom-call.6 = f32[4,128,128]{1,2,0:T(8,128)} custom-call(f32[4,128,128]{2,1,0:T(8,128)} %get-tuple-element.29), custom_call_target="InvertDiagBlocksLowerTriangular" | custom-call | tf_op jit(solution)/shard_map/triangular_solve/custom-call.1 | solution.py:26
  82.6 1.5 fusion.62
  85.3 0.7 convolution_subtract_fusion.3
  86.7 1.1 fusion.33
  88.5 1.6 maximum_select_fusion
  90.1 0.9 copy-done.11
  91.0 0.8 copy.12
  91.9 1.8 copy.6
  93.7 1.4 fusion.37
  95.2 7.4 %while.9 = (s32[]{:T(128)}, f32[512,512]{1,0:T(8,128)S(1)}, s32[4,2]{0,1:T(2,128)S(1)}, f32[4,128,128]{2,1,0:T(8,128)S(1)}, s32[]{:T(128)}) while((s32[]{:T(128)}, f32[512,512]{1,0:T(8,128)S(1)}, s32[4,2]{0,1:T(2,128)S(1)}, f32[4,128,128]{2,1,0:T(8,128)S(1)}, s32[]{:T(128)}) %tuple.99), condition=%wide.while_cond.clone, body=%wide.while_body.clone.sunk | while | flops 2 | bytes 131189 | solution.py:26
  95.8 1.2 bitcast_dynamic-update-slice_fusion.9
  97.6 1.2 bitcast_dynamic-update-slice_fusion.9
  99.5 1.2 bitcast_dynamic-update-slice_fusion.9
  101.3 1.2 bitcast_dynamic-update-slice_fusion.9
  102.6 40.4 %custom-call.7 = f32[4,128,128]{1,2,0:T(8,128)} custom-call(f32[4,128,128]{2,1,0:T(8,128)S(1)} %get-tuple-element.30), custom_call_target="InvertDiagBlocksLowerTriangular" | custom-call | tf_op jit(solution)/shard_map/triangular_solve/custom-call.1 | solution.py:26
  143.0 49.6 %all-reduce.5.cloned.1.call-done = f32[512,1024]{1,0:T(8,128)} async-done(((f32[512,1024]{1,0:T(8,128)}), f32[512,1024]{1,0:T(8,128)}) %all-reduce.5.cloned.1.call-update) | async-done | bytes 2097168 | tf_op jit(solution)/shard_map/psum | solution.py:9
  192.6 8.9 %bitcast_subtract_fusion.3 = f32[1,512,1024]{1,2,0:T(8,128)S(1)} fusion(f32[1,512,1024]{1,2,0:T(8,128)} %copy.6, f32[512,1024]{1,0:T(8,128)} %all-reduce.5.cloned.1.call-done, f32[1,1,512,512]{2,3,1,0:T(8,128)S(1)} %copy-done.9, pred[]{:T(512)S(6)} %gt.16), kind=kOutput, calls=%fused_computation.20 | convolution fusion | flops 3222274048 | bytes 7340033 | tf_op jit(solution)/shard_map/rcq,cx->rqx/dot_general | solution.py:29
  202.2 1.8 convolution_subtract_fusion.6
  204.7 2.8 convolution_subtract_fusion.2
  208.1 3.9 fusion.30
  212.7 1.6 maximum_select_fusion.1
  214.3 0.9 copy.13
  215.3 2.3 fusion.38
  217.7 12.0 %while.10 = (s32[]{:T(128)}, f32[512,512]{1,0:T(8,128)}, s32[4,2]{0,1:T(2,128)S(1)}, f32[4,128,128]{2,1,0:T(8,128)S(1)}, s32[]{:T(128)}) while((s32[]{:T(128)}, f32[512,512]{1,0:T(8,128)}, s32[4,2]{0,1:T(2,128)S(1)}, f32[4,128,128]{2,1,0:T(8,128)S(1)}, s32[]{:T(128)}) %tuple.100), condition=%wide.while_cond.clone.1, body=%wide.while_body.clone.1.sunk | while | flops 2 | bytes 131189 | solution.py:26
  218.4 2.3 bitcast_dynamic-update-slice_fusion.10
  221.4 2.3 bitcast_dynamic-update-slice_fusion.10
  224.4 2.3 bitcast_dynamic-update-slice_fusion.10
  227.4 2.2 bitcast_dynamic-update-slice_fusion.10
  229.7 0.7 copy-done.15
  230.4 40.1 %custom-call.8 = f32[4,128,128]{1,2,0:T(8,128)S(1)} custom-call(f32[4,128,128]{2,1,0:T(8,128)} %copy-done.15), custom_call_target="InvertDiagBlocksLowerTriangular" | custom-call | tf_op jit(solution)/shard_map/triangular_solve/custom-call.1 | solution.py:26
  270.5 46.1 %all-reduce.7.cloned.1.call-done = f32[512,1024]{1,0:T(8,128)} async-done(((f32[512,1024]{1,0:T(8,128)}), f32[512,1024]{1,0:T(8,128)}) %all-reduce.7.cloned.1.call-update) | async-done | bytes 2097168 | tf_op jit(solution)/shard_map/psum | solution.py:9
  316.6 8.3 %bitcast_subtract_fusion.2 = f32[1,512,1024]{1,2,0:T(8,128)S(1)} fusion(f32[1,512,1024]{1,2,0:T(8,128)S(1)} %bitcast_subtract_fusion.3, f32[512,1024]{1,0:T(8,128)} %all-reduce.7.cloned.1.call-done, f32[1,1,512,512]{2,3,1,0:T(8,128)S(1)} %copy-done.6, pred[]{:T(512)S(6)} %gt.17), kind=kOutput, calls=%fused_computation.19 | convolution fusion | flops 3222274048 | bytes 7340033 | tf_op jit(solution)/shard_map/rcq,cx->rqx/dot_general | solution.py:29
  325.6 1.9 convolution_subtract_fusion.5
  328.2 2.8 convolution_subtract_fusion.1
  331.6 4.1 fusion.27
  336.4 1.6 maximum_select_fusion.2
  338.1 2.6 fusion.39
  340.7 11.2 %while.11 = (s32[]{:T(128)}, f32[512,512]{1,0:T(8,128)}, s32[4,2]{0,1:T(2,128)S(1)}, f32[4,128,128]{2,1,0:T(8,128)S(1)}, s32[]{:T(128)}) while((s32[]{:T(128)}, f32[512,512]{1,0:T(8,128)}, s32[4,2]{0,1:T(2,128)S(1)}, f32[4,128,128]{2,1,0:T(8,128)S(1)}, s32[]{:T(128)}) %tuple.101), condition=%wide.while_cond.clone.2, body=%wide.while_body.clone.2.sunk | while | flops 2 | bytes 131189 | solution.py:26
  341.3 2.2 bitcast_dynamic-update-slice_fusion.11
  344.1 2.2 bitcast_dynamic-update-slice_fusion.11
  346.9 2.2 bitcast_dynamic-update-slice_fusion.11
  349.8 2.1 bitcast_dynamic-update-slice_fusion.11
  352.6 40.1 %custom-call.9 = f32[4,128,128]{1,2,0:T(8,128)S(1)} custom-call(f32[4,128,128]{2,1,0:T(8,128)} %copy-done.14), custom_call_target="InvertDiagBlocksLowerTriangular" | custom-call | tf_op jit(solution)/shard_map/triangular_solve/custom-call.1 | solution.py:26
  392.7 48.1 %all-reduce.9.cloned.1.call-done = f32[512,1024]{1,0:T(8,128)} async-done(((f32[512,1024]{1,0:T(8,128)}), f32[512,1024]{1,0:T(8,128)}) %all-reduce.9.cloned.1.call-update) | async-done | bytes 2097168 | tf_op jit(solution)/shard_map/psum | solution.py:9
  440.8 8.3 %bitcast_subtract_fusion.1 = f32[1,512,1024]{1,2,0:T(8,128)S(1)} fusion(f32[1,512,1024]{1,2,0:T(8,128)S(1)} %copy-done.1, f32[512,1024]{1,0:T(8,128)} %all-reduce.9.cloned.1.call-done, f32[1,1,512,512]{2,3,1,0:T(8,128)S(1)} %copy-done.7, pred[]{:T(512)S(6)} %gt.18), kind=kOutput, calls=%fused_computation.18 | convolution fusion | flops 3222274048 | bytes 7340033 | tf_op jit(solution)/shard_map/rcq,cx->rqx/dot_general | solution.py:29
  449.8 1.9 convolution_subtract_fusion.4
  452.4 2.8 convolution_subtract_fusion
  455.8 3.9 fusion.24
  460.3 1.6 maximum_select_fusion.3
  461.9 101.7 %all-reduce.11.cloned.1.call-done = f32[512,1024]{1,0:T(8,128)} async-done(((f32[512,1024]{1,0:T(8,128)}), f32[512,1024]{1,0:T(8,128)}) %all-reduce.11.cloned.1.call-update) | async-done | bytes 2097168 | tf_op jit(solution)/shard_map/psum | solution.py:9
  563.6 9.6 %bitcast_subtract_fusion = f32[1,512,1024]{1,2,0:T(8,128)} fusion(f32[1,512,1024]{1,2,0:T(8,128)S(1)} %copy-done.3, f32[512,1024]{1,0:T(8,128)} %all-reduce.11.cloned.1.call-done, f32[1,1,512,512]{2,3,1,0:T(8,128)S(1)} %copy-done.8, pred[]{:T(512)S(6)} %gt.19), kind=kOutput, calls=%fused_computation.17 | convolution fusion | flops 3222274048 | bytes 7340033 | tf_op jit(solution)/shard_map/rcq,cx->rqx/dot_general | solution.py:29
  573.2 3.0 copy.9
  576.3 5.8 pad_maximum_fusion
  (102 shorter events, 21.4 us)
Async XLA Ops:
  7.2 22.6 %all-gather.13.cloned.1.call-start = ((), (), s32[]{:S(2)}) async-start(), calls=%async_computation.4 | async-start | bytes 1310720 | tf_op jit(solution)/shard_map/all_gather | solution.py:24
  10.0 72.5 %copy-start.4 = (f32[1,512,1024]{2,1,0:T(8,128)S(1)}, f32[1,512,1024]{2,1,0:T(8,128)}, u32[]{:S(2)}) copy-start(f32[1,512,1024]{2,1,0:T(8,128)} %param.5) | copy-start | bytes 6291460
  10.1 83.6 %all-gather.15.cloned.1.call-start = ((), (), s32[]{:S(2)}) async-start(), calls=%async_computation.5 | async-start | bytes 1310720 | tf_op jit(solution)/shard_map/all_gather | solution.py:24
  11.0 181.6 %all-reduce.5.cloned.1.call-start = ((), (), s32[]{:S(2)}) async-start(), calls=%async_computation | async-start | bytes 4194304 | tf_op jit(solution)/shard_map/psum | solution.py:9
  82.6 2.1 copy-start.13
  90.0 0.9 copy-start.11
  90.0 125.3 %all-gather.17.cloned.1.call-start = ((), (), s32[]{:S(2)}) async-start(), calls=%async_computation.6 | async-start | bytes 1310720 | tf_op jit(solution)/shard_map/all_gather | solution.py:24
  91.8 224.8 %all-reduce.7.cloned.1.call-start = ((), (), s32[]{:S(2)}) async-start(), calls=%async_computation.1 | async-start | bytes 4194304 | tf_op jit(solution)/shard_map/psum | solution.py:9
  93.7 98.9 %copy-start.9 = (f32[1,1,512,512]{2,3,1,0:T(8,128)S(1)}, f32[1,1,512,512]{2,3,1,0:T(8,128)}, u32[]{:S(2)}) copy-start(f32[1,1,512,512]{2,3,1,0:T(8,128)} %all-gather.13.cloned.1.call-done) | copy-start | bytes 3145732
  102.6 40.4 %copy-start.10 = (f32[512,512]{1,0:T(8,128)}, f32[512,512]{1,0:T(8,128)S(1)}, u32[]{:S(2)}) copy-start(f32[512,512]{1,0:T(8,128)S(1)} %get-tuple-element.280) | copy-start | bytes 3145732
  192.6 8.9 %copy-start.12 = (f32[4,128,128]{1,2,0:T(8,128)S(1)}, f32[4,128,128]{1,2,0:T(8,128)}, u32[]{:S(2)}) copy-start(f32[4,128,128]{1,2,0:T(8,128)} %custom-call.7) | copy-start | bytes 786436
  214.3 102.4 %copy-start.6 = (f32[1,1,512,512]{2,3,1,0:T(8,128)S(1)}, f32[1,1,512,512]{2,3,1,0:T(8,128)}, u32[]{:S(2)}) copy-start(f32[1,1,512,512]{2,3,1,0:T(8,128)} %all-gather.15.cloned.1.call-done) | copy-start | bytes 3145732
  214.3 123.8 %all-gather.19.cloned.1.call-start = ((), (), s32[]{:S(2)}) async-start(), calls=%async_computation.7 | async-start | bytes 1310720 | tf_op jit(solution)/shard_map/all_gather | solution.py:24
  215.2 225.6 %all-reduce.9.cloned.1.call-start = ((), (), s32[]{:S(2)}) async-start(), calls=%async_computation.2 | async-start | bytes 4194304 | tf_op jit(solution)/shard_map/psum | solution.py:9
  229.7 0.7 copy-start.15
  324.9 6.7 %copy-start = (f32[1,512,1024]{1,2,0:T(8,128)}, f32[1,512,1024]{1,2,0:T(8,128)S(1)}, u32[]{:S(2)}) copy-start(f32[1,512,1024]{1,2,0:T(8,128)S(1)} %bitcast_subtract_fusion.2) | copy-start | bytes 6291460
  337.9 102.9 %copy-start.7 = (f32[1,1,512,512]{2,3,1,0:T(8,128)S(1)}, f32[1,1,512,512]{2,3,1,0:T(8,128)}, u32[]{:S(2)}) copy-start(f32[1,1,512,512]{2,3,1,0:T(8,128)} %all-gather.17.cloned.1.call-done) | copy-start | bytes 3145732
  338.0 102.9 %copy-start.1 = (f32[1,512,1024]{1,2,0:T(8,128)S(1)}, f32[1,512,1024]{1,2,0:T(8,128)}, u32[]{:S(2)}) copy-start(f32[1,512,1024]{1,2,0:T(8,128)} %copy-done) | copy-start | bytes 6291460
  338.0 225.7 %all-reduce.11.cloned.1.call-start = ((), (), s32[]{:S(2)}) async-start(), calls=%async_computation.3 | async-start | bytes 4194304 | tf_op jit(solution)/shard_map/psum | solution.py:9
  351.9 0.7 copy-start.14
  449.1 6.6 %copy-start.2 = (f32[1,512,1024]{1,2,0:T(8,128)}, f32[1,512,1024]{1,2,0:T(8,128)S(1)}, u32[]{:S(2)}) copy-start(f32[1,512,1024]{1,2,0:T(8,128)S(1)} %bitcast_subtract_fusion.1) | copy-start | bytes 6291460
  460.3 103.3 %copy-start.8 = (f32[1,1,512,512]{2,3,1,0:T(8,128)S(1)}, f32[1,1,512,512]{2,3,1,0:T(8,128)}, u32[]{:S(2)}) copy-start(f32[1,1,512,512]{2,3,1,0:T(8,128)} %all-gather.19.cloned.1.call-done) | copy-start | bytes 3145732
  461.9 101.8 %copy-start.3 = (f32[1,512,1024]{1,2,0:T(8,128)S(1)}, f32[1,512,1024]{1,2,0:T(8,128)}, u32[]{:S(2)}) copy-start(f32[1,512,1024]{1,2,0:T(8,128)} %copy-done.2) | copy-start | bytes 6291460
  573.2 3.0 copy-start.5
Sparse Core Ops, SparseCore 0:
  10.2 19.5 all-gather.12
  31.3 16.9 all-gather.14
  90.2 102.4 all-reduce.4
  194.0 16.0 all-gather.16
  214.4 102.1 all-reduce.6
  318.0 16.0 all-gather.18
  338.3 102.4 all-reduce.8
  462.0 101.5 all-reduce.10
where the time goes:
time: 598 us; the launch traced here: 589 us
  waiting for transfers between devices  264 us (44%)
  other arithmetic  181 us (30%)
  matrix products  74.5 us (12%)
  local copies, waits for them, and re-layouts  53.6 us (9%)
  between operations  14.8 us (2%)
    psum x4, waiting for transfers between devices, from_root(): return lax.psum(jnp.where(mine, x, jnp.zeros_like(x)), axis)  246 us
    another operation x9, other arithmetic, per_device(): lax.linalg.triangular_solve(safe_tile, current[0], left_side=True, lower=...  169 us
    another operation x53, local copies, waits for them, and re-layouts, per_device(): lax.linalg.triangular_solve(safe_tile, current[0], left_side=True, lower=...  41.1 us
    another operation x28, matrix products, per_device(): lax.linalg.triangular_solve(safe_tile, current[0], left_side=True, lower=...  39.4 us
    dot_general x4, matrix products, per_device(): jnp.einsum('rcq,cx->rqx', lax.all_gather(column, 'col', axis=1, tiled=Tru...  35.1 us
    all_gather x4, waiting for transfers between devices, per_device(): diag_tile = lax.all_gather(column[0], 'col', axis=0, tiled=True).T  18.7 us
  transfers between devices with their start and end apart: 8, of which 5 were waited for; matrix products, arithmetic and copies ran while one was open for 45% of the time, Pallas kernels for 0%

commit v1 on v0

--- a/solution.py
+++ b/solution.py
@@ -4,9 +4,13 @@
 from jax.sharding import PartitionSpec as P
 
 
+def bring_columns(field_in, which_axis):
+    return lax.all_gather(field_in, which_axis).sum(axis=0)
+
+
 def from_root(x, axis, root):
     mine = lax.axis_index(axis) == root
-    return lax.psum(jnp.where(mine, x, jnp.zeros_like(x)), axis)
+    return bring_columns(jnp.where(mine, x, jnp.zeros_like(x)), axis)
 
 
 def per_device(lower_panel, right_side):

time: 598 us -> 1130 us (1.89)
  waiting for transfers between devices: 264 us -> 768 us
  other arithmetic: 181 us -> 216 us
    all_gather x0 -> x4, waiting for transfers between devices: none -> 750 us  [bring_columns(): return lax.all_gather(field_in, which_axis).sum(axis=0)]
    psum x4 -> x0, waiting for transfers between devices: 246 us -> none  [from_root(): return lax.psum(jnp.where(mine, x, jnp.zeros_like(x)), axis)]
    reduce_sum x0 -> x4, other arithmetic: none -> 37.8 us  [bring_columns(): return lax.all_gather(field_in, which_axis).sum(axis=0)]
  transfers between devices with their start and end apart: 8 -> 8, of which waited for: 5 -> 5; matrix products, arithmetic and copies ran while one was open for 45% -> 25% of each run, Pallas kernels for 0% -> 0%
where the time goes in v1:
time: 1130 us; the launch traced here: 1120 us
  waiting for transfers between devices  768 us (68%)
  other arithmetic  216 us (19%)
  matrix products  74.4 us (7%)
  local copies, waits for them, and re-layouts  47.5 us (4%)
  between operations  15.1 us (1%)
    all_gather x4, waiting for transfers between devices, bring_columns(): return lax.all_gather(field_in, which_axis).sum(axis=0)  750 us
    another operation x9, other arithmetic, per_device(): lax.linalg.triangular_solve(safe_tile, current[0], left_side=True, lower=...  166 us
    another operation x28, matrix products, per_device(): lax.linalg.triangular_solve(safe_tile, current[0], left_side=True, lower=...  39.2 us
    reduce_sum x4, other arithmetic, bring_columns(): return lax.all_gather(field_in, which_axis).sum(axis=0)  37.8 us
    another operation x53, local copies, waits for them, and re-layouts, per_device(): lax.linalg.triangular_solve(safe_tile, current[0], left_side=True, lower=...  35.7 us
    dot_general x4, matrix products, per_device(): jnp.einsum('rcq,cx->rqx', lax.all_gather(column, 'col', axis=1, tiled=Tru...  35.2 us
  transfers between devices with their start and end apart: 8, of which 5 were waited for; matrix products, arithmetic and copies ran while one was open for 25% of the time, Pallas kernels for 0%

profile of v1, /device:TPU:0, one launch (start us, length us, event | category | flops | bytes accessed | tf_op | source)
XLA Modules:
  0.0 1122.1 jit_solution(10997522285641688633)
XLA Ops:
  7.2 2.0 fusion.100
  9.2 0.8 copy.10
  10.1 0.8 copy.11
  11.0 18.7 %all-gather.21.cloned.1.call-done = f32[1,1,512,512]{2,3,1,0:T(8,128)} async-done(((f32[1,1,128,512]{2,3,1,0:T(8,128)}), f32[1,1,512,512]{2,3,1,0:T(8,128)}) %all-gather.21.cloned.1.call-update) | async-done | bytes 1048592 | tf_op jit(solution)/shard_map/all_gather | solution.py:28
  29.8 1.4 fusion.36
  31.9 10.4 while.8
  32.5 1.9 bitcast_dynamic-update-slice_fusion.8
  35.1 1.9 bitcast_dynamic-update-slice_fusion.8
  37.7 1.9 bitcast_dynamic-update-slice_fusion.8
  40.3 1.9 bitcast_dynamic-update-slice_fusion.8
  42.2 40.7 %custom-call.6 = f32[4,128,128]{1,2,0:T(8,128)} custom-call(f32[4,128,128]{2,1,0:T(8,128)} %get-tuple-element.29), custom_call_target="InvertDiagBlocksLowerTriangular" | custom-call | tf_op jit(solution)/shard_map/triangular_solve/custom-call.1 | solution.py:30
  83.0 1.5 fusion.62
  87.1 1.1 fusion.33
  88.9 1.6 maximum_select_fusion
  90.5 0.9 copy-done.13
  92.3 1.8 copy.6
  94.1 1.4 fusion.37
  95.5 8.6 while.9
  96.2 1.5 bitcast_dynamic-update-slice_fusion.9
  98.3 1.5 bitcast_dynamic-update-slice_fusion.9
  100.5 1.5 bitcast_dynamic-update-slice_fusion.9
  102.6 1.5 bitcast_dynamic-update-slice_fusion.9
  104.1 40.1 %custom-call.7 = f32[4,128,128]{1,2,0:T(8,128)} custom-call(f32[4,128,128]{2,1,0:T(8,128)S(1)} %get-tuple-element.30), custom_call_target="InvertDiagBlocksLowerTriangular" | custom-call | tf_op jit(solution)/shard_map/triangular_solve/custom-call.1 | solution.py:30
  144.2 173.7 %all-gather.23.cloned.1.call-done = f32[4096,1024]{1,0:T(8,128)} async-done(((f32[512,1024]{1,0:T(8,128)}), f32[4096,1024]{1,0:T(8,128)}) %all-gather.23.cloned.1.call-update) | async-done | bytes 16777232 | tf_op jit(solution)/shard_map/all_gather | solution.py:8
  317.9 9.4 reduce_sum.36
  327.3 8.9 bitcast_subtract_fusion.3
  336.9 1.8 convolution_subtract_fusion.6
  339.4 3.0 convolution_subtract_fusion.2
  343.0 3.7 fusion.30
  347.4 1.6 maximum_select_fusion.1
  349.0 0.8 copy.13
  350.0 1.4 fusion.38
  351.4 8.1 while.10
  352.0 1.4 bitcast_dynamic-update-slice_fusion.10
  354.0 1.4 bitcast_dynamic-update-slice_fusion.10
  356.1 1.4 bitcast_dynamic-update-slice_fusion.10
  358.1 1.4 bitcast_dynamic-update-slice_fusion.10
  360.2 40.6 %custom-call.8 = f32[4,128,128]{1,2,0:T(8,128)S(1)} custom-call(f32[4,128,128]{2,1,0:T(8,128)} %copy-done.16), custom_call_target="InvertDiagBlocksLowerTriangular" | custom-call | tf_op jit(solution)/shard_map/triangular_solve/custom-call.1 | solution.py:30
  400.7 173.8 %all-gather.27.cloned.1.call-done = f32[4096,1024]{1,0:T(8,128)} async-done(((f32[512,1024]{1,0:T(8,128)}), f32[4096,1024]{1,0:T(8,128)}) %all-gather.27.cloned.1.call-update) | async-done | bytes 16777232 | tf_op jit(solution)/shard_map/all_gather | solution.py:8
  574.6 9.5 reduce_sum.37
  584.0 8.3 bitcast_subtract_fusion.2
  593.0 1.9 convolution_subtract_fusion.5
  595.6 2.9 convolution_subtract_fusion.1
  599.2 3.7 fusion.27
  603.5 1.6 maximum_select_fusion.2
  605.2 1.4 fusion.39
  606.6 8.1 while.11
  607.3 1.3 bitcast_dynamic-update-slice_fusion.11
  609.3 1.3 bitcast_dynamic-update-slice_fusion.11
  611.3 1.3 bitcast_dynamic-update-slice_fusion.11
  613.4 1.3 bitcast_dynamic-update-slice_fusion.11
  614.7 39.5 %custom-call.9 = f32[4,128,128]{1,2,0:T(8,128)S(1)} custom-call(f32[4,128,128]{2,1,0:T(8,128)S(1)} %get-tuple-element.32), custom_call_target="InvertDiagBlocksLowerTriangular" | custom-call | tf_op jit(solution)/shard_map/triangular_solve/custom-call.1 | solution.py:30
  654.3 176.4 %all-gather.31.cloned.1.call-done = f32[4096,1024]{1,0:T(8,128)} async-done(((f32[512,1024]{1,0:T(8,128)}), f32[4096,1024]{1,0:T(8,128)}) %all-gather.31.cloned.1.call-update) | async-done | bytes 16777232 | tf_op jit(solution)/shard_map/all_gather | solution.py:8
  830.7 9.4 reduce_sum.38
  840.2 8.3 bitcast_subtract_fusion.1
  849.2 1.9 convolution_subtract_fusion.4
  851.7 3.0 convolution_subtract_fusion
  855.4 3.7 fusion.24
  859.7 1.6 maximum_select_fusion.3
  861.3 225.6 %all-gather.35.cloned.1.call-done = f32[4096,1024]{1,0:T(8,128)} async-done(((f32[512,1024]{1,0:T(8,128)}), f32[4096,1024]{1,0:T(8,128)}) %all-gather.35.cloned.1.call-update) | async-done | bytes 16777232 | tf_op jit(solution)/shard_map/all_gather | solution.py:8
  1086.9 9.5 reduce_sum.39
  1096.4 9.6 bitcast_subtract_fusion
  1106.1 3.0 copy.9
  1109.1 5.8 pad_maximum_fusion
  (108 shorter events, 24.3 us)
Async XLA Ops:
  7.2 22.6 %all-gather.21.cloned.1.call-start = ((), (), s32[]{:S(2)}) async-start(), calls=%async_computation | async-start | bytes 1310720 | tf_op jit(solution)/shard_map/all_gather | solution.py:28
  10.0 72.9 %copy-start.5 = (f32[1,512,1024]{2,1,0:T(8,128)S(1)}, f32[1,512,1024]{2,1,0:T(8,128)}, u32[]{:S(2)}) copy-start(f32[1,512,1024]{2,1,0:T(8,128)} %param.5) | copy-start | bytes 6291460
  10.1 84.0 %all-gather.25.cloned.1.call-start = ((), (), s32[]{:S(2)}) async-start(), calls=%async_computation.2 | async-start | bytes 1310720 | tf_op jit(solution)/shard_map/all_gather | solution.py:28
  11.0 306.9 %all-gather.23.cloned.1.call-start = ((), (), s32[]{:S(2)}) async-start(), calls=%async_computation.1 | async-start | bytes 18874368 | tf_op jit(solution)/shard_map/all_gather | solution.py:8
  83.0 2.1 copy-start.15
  90.4 0.9 copy-start.13
  90.5 259.5 %all-gather.29.cloned.1.call-start = ((), (), s32[]{:S(2)}) async-start(), calls=%async_computation.4 | async-start | bytes 1310720 | tf_op jit(solution)/shard_map/all_gather | solution.py:28
  92.2 482.4 %all-gather.27.cloned.1.call-start = ((), (), s32[]{:S(2)}) async-start(), calls=%async_computation.3 | async-start | bytes 18874368 | tf_op jit(solution)/shard_map/all_gather | solution.py:8
  104.1 213.8 %copy-start.11 = (f32[512,512]{1,0:T(8,128)}, f32[512,512]{1,0:T(8,128)S(1)}, u32[]{:S(2)}) copy-start(f32[512,512]{1,0:T(8,128)S(1)} %get-tuple-element.280) | copy-start | bytes 3145732
  317.9 9.4 copy-start.9
  327.3 8.9 copy-start.14
  349.0 256.2 %all-gather.33.cloned.1.call-start = ((), (), s32[]{:S(2)}) async-start(), calls=%async_computation.6 | async-start | bytes 1310720 | tf_op jit(solution)/shard_map/all_gather | solution.py:28
  349.9 480.8 %all-gather.31.cloned.1.call-start = ((), (), s32[]{:S(2)}) async-start(), calls=%async_computation.5 | async-start | bytes 18874368 | tf_op jit(solution)/shard_map/all_gather | solution.py:8
  359.5 0.7 copy-start.16
  360.2 214.4 %copy-start.12 = (f32[512,512]{1,0:T(8,128)}, f32[512,512]{1,0:T(8,128)S(1)}, u32[]{:S(2)}) copy-start(f32[512,512]{1,0:T(8,128)S(1)} %get-tuple-element.281) | copy-start | bytes 3145732
  574.6 9.5 copy-start.6
  592.4 6.8 copy-start
  605.1 481.8 %all-gather.35.cloned.1.call-start = ((), (), s32[]{:S(2)}) async-start(), calls=%async_computation.7 | async-start | bytes 18874368 | tf_op jit(solution)/shard_map/all_gather | solution.py:8
  614.7 216.0 %copy-start.10 = (f32[512,512]{1,0:T(8,128)}, f32[512,512]{1,0:T(8,128)S(1)}, u32[]{:S(2)}) copy-start(f32[512,512]{1,0:T(8,128)S(1)} %get-tuple-element.279) | copy-start | bytes 3145732
  830.7 9.4 copy-start.1
  830.7 9.4 copy-start.7
  848.5 6.9 copy-start.2
  1086.9 9.5 copy-start.3
  1086.9 9.5 copy-start.8
  1106.1 3.0 copy-start.4
Sparse Core Ops, SparseCore 0:
  10.2 19.5 all-gather.20
  31.3 16.8 all-gather.24
  90.6 227.2 all-gather.22
  319.3 14.9 all-gather.28
  349.1 225.4 all-gather.26
  576.0 14.9 all-gather.32
  605.2 225.4 all-gather.30
  861.4 225.4 all-gather.34
